TPU v7x, 1024 devices: a whole 4x8x16 slice. The times are simulated.
1024 devices in a mesh: gx: 64 (over x_hi, z, core), gy: 16 (over y, x_lo).
Axes of the slice: x: 4 (x_hi: 2, x_lo: 2; x = x_hi * 2 + x_lo), y: 8, z: 16, core: 2. Of those that a mesh axis runs over, the one named last changes fastest.
Arguments:
- density: float32 [1024, 768, 128], P('gx', 'gy'), may hold values from -6 to 6
- momenta: float32 [3, 1024, 768, 128], P(None, 'gx', 'gy'), may hold values from -6 to 6
- smooth_taps: float32 [33], replicated, may hold values from -1 to 1
- deriv_taps: float32 [33], replicated, may hold values from -1 to 1
- kick_step: float32 [], replicated, may hold values from 0.5 to 1.5
Outputs:
- kicked: float32 [3, 1024, 768, 128], P(None, 'gx', 'gy')
All inputs are finite; a program needn't handle non-finite values.
Results may differ from a plain program's by a relative error of at most 0.00007.
Values sent between devices are 32-bit elements; how exact they have to be, the bound alone decides.
A program may use at most 64 MiB of HBM per device.

v0:
```python
import functools
import math

import jax
import jax.numpy as jnp
import numpy as np
from jax import lax
from jax.experimental import pallas as pl
from jax.experimental.pallas import tpu as pltpu
from jax.sharding import PartitionSpec as P

FACTOR = 4
RADIUS = 16
LONG_COUPLING = 16.0
HIGHEST = lax.Precision.HIGHEST
MESH = pl.DeviceIdType.MESH
F32 = jnp.float32

T_P, T_Q, T_A, T_B, T_C, T_G, T_W, T_ROWS = 0, 16, 32, 64, 96, 128, 176, 184
C_ZF, C_ZI, C_ZD, C_YF, C_YI, C_ROWS = 0, 32, 64, 96, 608, 1120


def z_basis():
    n = np.arange(32)
    basis = np.zeros((2, 16, 32))
    norm = np.full((2, 16), 2.0 / 32)
    for g in range(16):
        basis[0, g] = np.cos(2 * np.pi * g * n / 32)
        basis[1, g] = np.sin(2 * np.pi * g * n / 32)
    basis[1, 0] = np.cos(np.pi * n)
    norm[:, 0] = 1.0 / 32
    return basis.reshape(32, 32), norm.reshape(32)


def y_basis(count):
    half = count // 2
    wave = np.array([m if m <= half else m - half for m in range(count)])
    y = np.arange(count)
    angle = 2 * np.pi / count * (wave[:, None] * y[None, :] % count)
    is_cos = (np.arange(count) <= half)[:, None]
    basis = np.where(is_cos, np.cos(angle), np.sin(angle))
    norm = np.where((wave == 0) | (wave == half), 1.0, 2.0) / count
    return basis, norm, wave


def shared_constants():
    out = np.zeros((C_ROWS, 128))
    zb, zn = z_basis()
    out[C_ZF : C_ZF + 32] = np.repeat(zb, 4, axis=1) / 64.0
    zi = zb * zn[:, None] * LONG_COUPLING
    out[C_ZI : C_ZI + 32] = np.repeat(zi, 4, axis=1)
    zd = 0.5 * (np.roll(zi, -1, axis=1) - np.roll(zi, 1, axis=1))
    out[C_ZD : C_ZD + 32] = np.repeat(zd, 4, axis=1)
    yb, yn, _ = y_basis(192)
    for tile in range(2):
        for half in range(2):
            fwd = np.zeros((128, 128))
            inv = np.zeros((128, 128))
            fwd[:96, :96] = yb[96 * half : 96 * half + 96, 96 * tile : 96 * tile + 96].T
            for jj in range(8):
                for p in range(14):
                    y = (12 * (8 * tile + jj) - 1 + p) % 192
                    cols = slice(96 * half, 96 * half + 96)
                    inv[:96, 16 * jj + p] = yb[cols, y] * yn[cols]
            row = C_YF + (2 * tile + half) * 128
            out[row : row + 128] = fwd
            row = C_YI + (2 * half + tile) * 128
            out[row : row + 128] = inv
    return out.astype(np.float32)


def solve_tables(chips):
    n = 8 * chips
    out = np.zeros((16, 2, T_ROWS, 128))
    _, _, wave = y_basis(192)
    for g in range(16):
        for half in range(2):
            t = out[g, half]
            ky = wave[96 * half : 96 * half + 96]
            for c in range(2):
                kz = 16 if (g == 0 and c == 1) else g
                a = np.ones(128)
                a[:96] = (2 - 2 * np.cos(2 * np.pi * ky / 192)) + (2 - 2 * np.cos(2 * np.pi * kz / 32))
                zero = np.zeros(128, bool)
                zero[:96] = (ky == 0) & (kz == 0)
                a[zero] = 1.0
                r = 1 + a / 2 - np.sqrt(a + a * a / 4)
                den = (1 / r - r) * (1 - r**n)
                pick = lambda general, special: np.where(zero, special, general)
                for sc in range(2):
                    for xl in range(4):
                        x8 = 4 * sc + xl
                        t[T_P + sc * 8 + c * 4 + xl] = pick(r ** (-x8), 1.0)
                        t[T_Q + sc * 8 + c * 4 + xl] = pick(r**x8, float(x8))
                for ct in range(2):
                    for i in range(6):
                        x8 = 4 * ct - 1 + i
                        row = ct * 16 + c * 8 + i
                        t[T_A + row] = pick(r ** float(x8) / den, -x8 / 2 + x8 * x8 / (2 * n))
                        t[T_B + row] = pick(r ** float(-x8) / den, -x8 / n)
                        t[T_C + row] = pick(0.0, 8 * x8 / n)
                for o in range(17):
                    d = abs(o - 8)
                    t[T_G + c * 24 + o] = pick((r**d + r ** (n - d)) / den, -d * (n - d) / (2 * n))
                for pq in range(2):
                    t[T_W + pq * 2 + c] = pick(r**8, 1.0)
    return out.reshape(32, T_ROWS, 128).astype(np.float32)


def dot(a, b):
    return lax.dot_general(a, b, (((1,), (0,)), ((), ())), precision=HIGHEST, preferred_element_type=F32)


def dot_nt(a, b):
    return lax.dot_general(a, b, (((1,), (1,)), ((), ())), precision=HIGHEST, preferred_element_type=F32)


def wrap(value, count):
    return lax.rem(value + count, count)


def send_order(chips):
    ring = min(16, chips)
    def hops(step):
        along = step % ring
        return min(along, ring - along) + (2 if step >= ring else 0)
    return sorted(range(1, chips), key=lambda step: (-hops(step), step))


def kernel(
    gx_count, density, cst_hbm, tab_hbm, padded, long_ref,
    cst, tab, m1, r1, fs, pair, mom, r2, os_, pair2, ps, r3,
    load_sem, strip_send, strip_recv, tile_send, tile_recv, corner_send, corner_recv,
    m_send, m_recv, p_send, p_recv,
):
    gx = lax.axis_index("gx")
    gy = lax.axis_index("gy")
    chips = gx_count // 2
    core = lax.rem(gx, 2)
    chip = gx // 2
    partner = gx + 1 - 2 * core
    outer = wrap(gx + 2 * core - 1, gx_count)

    barrier = pltpu.get_barrier_semaphore()

    def greet(device):
        pl.semaphore_signal(barrier, inc=1, device_id=device, device_id_type=MESH)

    for step in send_order(chips):
        greet({"gx": 2 * lax.rem(chip + step, chips) + core})
    for step in range(1, 16):
        greet({"gy": lax.rem(gy + step, 16)})
    greet({"gx": outer})
    greet({"gx": partner})

    loads = [
        pltpu.make_async_copy(density, padded.at[16:32, 16:64], load_sem.at[0]),
        pltpu.make_async_copy(cst_hbm, cst, load_sem.at[1]),
        pltpu.make_async_copy(tab_hbm.at[2 * gy + core], tab, load_sem.at[2]),
    ]
    for load in loads:
        load.start()
    for load in loads:
        load.wait()

    lane = lax.broadcasted_iota(jnp.int32, (48, 128), 1)
    block = lax.broadcasted_iota(jnp.int32, (48, 128), 0) // 4
    placed = (lane == block + 12 * lax.rem(gy, 8)).astype(F32)
    zf = cst[C_ZF : C_ZF + 32]
    for xl in range(4):
        rows = padded[16 + 4 * xl, 16:64]
        for fine in range(1, 4):
            rows = rows + padded[16 + 4 * xl + fine, 16:64]
        spread = dot(dot_nt(zf, rows), placed)
        for c in range(2):
            m1[:, c * 4 + xl, :] = spread[16 * c : 16 * c + 16]

    pl.semaphore_wait(barrier, (chips - 1) + 15 + 2)

    def remote(src, dst, send_sem, recv_sem, device):
        return pltpu.make_async_remote_copy(
            src_ref=src, dst_ref=dst, send_sem=send_sem, recv_sem=recv_sem,
            device_id=device, device_id_type=MESH,
        )

    for step in (8, 7, 9, 6, 10, 5, 11, 4, 12, 3, 13, 2, 14, 1, 15):
        target = lax.rem(gy + step, 16)
        remote(m1.at[target], r1.at[gy], m_send.at[0], m_recv.at[0], {"gy": target}).start()
    below, above = wrap(gy - 1, 16), lax.rem(gy + 1, 16)
    strips = [
        remote(padded.at[16:32, 16:32], padded.at[16:32, 64:80], strip_send.at[0], strip_recv.at[0], {"gy": below}),
        remote(padded.at[16:32, 48:64], padded.at[16:32, 0:16], strip_send.at[1], strip_recv.at[1], {"gy": above}),
    ]
    back, ahead = wrap(gx - 1, gx_count), lax.rem(gx + 1, gx_count)
    tiles = [
        remote(padded.at[16:32, 16:64], padded.at[32:48, 16:64], tile_send.at[0], tile_recv.at[0], {"gx": back}),
        remote(padded.at[16:32, 16:64], padded.at[0:16, 16:64], tile_send.at[1], tile_recv.at[1], {"gx": ahead}),
    ]
    for copy in strips + tiles:
        copy.start()

    r1[gy] = m1[gy]
    pltpu.make_async_copy(r1.at[0:15], r1.at[0:15], m_recv.at[0]).wait()
    low = r1[0]
    high = r1[8]
    for j in range(1, 8):
        low = low + r1[j]
        high = high + r1[8 + j]
    for half in range(2):
        first = C_YF + half * 128
        second = C_YF + (2 + half) * 128
        fs[half] = dot(low, cst[first : first + 128]) + dot(high, cst[second : second + 128])
    swap = remote(fs.at[1 - core], pair.at[core], p_send.at[0], p_recv.at[0], {"gx": partner})
    swap.start()
    pair[core] = fs[core]
    swap.wait_recv()

    e0 = pair[0]
    e1 = pair[1]
    for pq, table in ((0, T_P), (1, T_Q)):
        terms = e0 * tab[table : table + 8] + e1 * tab[table + 8 : table + 16]
        for c in range(2):
            mom[2 * pq + c : 2 * pq + c + 1, :] = jnp.sum(terms[4 * c : 4 * c + 4], axis=0, keepdims=True)
    for step in send_order(chips):
        target = 2 * lax.rem(chip + step, chips) + core
        remote(mom, r2.at[step], m_send.at[1], m_recv.at[1], {"gx": target}).start()

    for copy in strips:
        copy.wait_recv()
    corners = []
    for side, cols in enumerate((slice(0, 16), slice(64, 80))):
        corners.append(remote(padded.at[16:32, cols], padded.at[32:48, cols], corner_send.at[2 * side], corner_recv.at[2 * side], {"gx": back}))
        corners.append(remote(padded.at[16:32, cols], padded.at[0:16, cols], corner_send.at[2 * side + 1], corner_recv.at[2 * side + 1], {"gx": ahead}))
    for copy in corners:
        copy.start()

    pltpu.make_async_copy(r2.at[1:chips], r2.at[1:chips], m_recv.at[1]).wait()
    ratio = tab[T_W : T_W + 4]
    is_first = lax.broadcasted_iota(jnp.int32, (4, 128), 0) < 2
    total = jnp.zeros((4, 128), F32)
    ramp = jnp.zeros((4, 128), F32)
    for step in range(chips - 1, 0, -1):
        total = (total + jnp.where(is_first, r2[step], r2[chips - step])) * ratio
        ramp = ramp + total
    for ct in range(2):
        for c in range(2):
            row = ct * 16 + c * 8
            phi = (
                tab[T_A + row : T_A + row + 8] * total[c : c + 1]
                + tab[T_B + row : T_B + row + 8] * total[2 + c : 3 + c]
                + tab[T_C + row : T_C + row + 8] * ramp[c : c + 1]
            )
            for x8 in range(8):
                source = (e0 if x8 < 4 else e1)[c * 4 + x8 % 4 : c * 4 + x8 % 4 + 1]
                start = T_G + c * 24 + 7 + 4 * ct - x8
                phi = phi + tab[start : start + 8] * source
            os_[ct, c * 8 : c * 8 + 8, :] = phi
    swap2 = remote(os_.at[1 - core], pair2.at[core], p_send.at[1], p_recv.at[1], {"gx": partner})
    swap2.start()
    pair2[core] = os_[core]
    swap2.wait_recv()

    h0 = pair2[0]
    h1 = pair2[1]
    for tile in range(2):
        first = C_YI + tile * 128
        second = C_YI + (2 + tile) * 128
        ps[tile] = dot(h0, cst[first : first + 128]) + dot(h1, cst[second : second + 128])
    for step in (8, 7, 9, 6, 10, 5, 11, 4, 12, 3, 13, 2, 14, 1, 15):
        target = lax.rem(gy + step, 16)
        remote(ps.at[target // 8], r3.at[gy], m_send.at[2], m_recv.at[2], {"gy": target}).start()
    r3[gy] = ps[gy // 8]

    for copy in tiles + corners:
        copy.wait_recv()

    pltpu.make_async_copy(r3.at[0:15], r3.at[0:15], m_recv.at[2]).wait()
    here = block + 16 * lax.rem(gy, 8) + 1
    at_cell = (lane == here).astype(F32)
    slope = 0.5 * (lane == here + 1).astype(F32) - 0.5 * (lane == here - 1).astype(F32)
    along = []
    across = []
    for i in range(6):
        coeffs = jnp.concatenate([r3[:, i, :], r3[:, 8 + i, :]], axis=0)
        along.append(dot_nt(at_cell, coeffs))
        if 1 <= i <= 4:
            across.append(dot_nt(slope, coeffs))
    zi = cst[C_ZI : C_ZI + 32]
    zd = cst[C_ZD : C_ZD + 32]
    for xl in range(4):
        long_ref[0, xl] = dot(0.5 * (along[xl + 2] - along[xl]), zi)
        long_ref[1, xl] = dot(across[xl], zi)
        long_ref[2, xl] = dot(along[xl + 1], zd)

    for copy in strips + tiles + corners + [swap, swap2]:
        copy.wait_send()
    pltpu.make_async_copy(m1.at[0:15], m1.at[0:15], m_send.at[0]).wait()
    pltpu.make_async_copy(r2.at[1:chips], r2.at[1:chips], m_send.at[1]).wait()
    pltpu.make_async_copy(r3.at[0:15], r3.at[0:15], m_send.at[2]).wait()


def exchange(density, gx_count):
    chips = gx_count // 2
    any_spec = pl.BlockSpec(memory_space=pl.ANY)
    vmem_spec = pl.BlockSpec(memory_space=pltpu.VMEM)
    vm = lambda *shape: pltpu.VMEM(shape, F32)
    dma = lambda n: pltpu.SemaphoreType.DMA((n,))
    return pl.pallas_call(
        functools.partial(kernel, gx_count),
        out_shape=(
            jax.ShapeDtypeStruct((48, 80, 128), F32),
            jax.ShapeDtypeStruct((3, 4, 48, 128), F32),
        ),
        in_specs=[any_spec] * 3,
        out_specs=(vmem_spec, vmem_spec),
        scratch_shapes=[
            vm(C_ROWS, 128), vm(T_ROWS, 128), vm(16, 8, 128), vm(16, 8, 128), vm(2, 8, 128), vm(2, 8, 128),
            vm(4, 128), vm(chips, 4, 128), vm(2, 16, 128), vm(2, 16, 128), vm(2, 16, 128), vm(16, 16, 128),
            dma(3), dma(2), dma(2), dma(2), dma(2), dma(4), dma(4), dma(3), dma(3), dma(2), dma(2),
        ],
        compiler_params=pltpu.CompilerParams(collective_id=0, has_side_effects=True),
    )(density, jnp.asarray(shared_constants()), jnp.asarray(solve_tables(chips)))


def band_matrix(weights, sources, targets, shift, period):
    source_idx = lax.broadcasted_iota(jnp.int32, (sources, targets), 0)
    target_idx = lax.broadcasted_iota(jnp.int32, (sources, targets), 1)
    offset = source_idx - target_idx + shift
    if period > 0:
        offset = offset % period
    tap_index = jnp.arange(weights.shape[0], dtype=jnp.int32)
    one_hot = (offset[:, :, None] == tap_index[None, None, :]).astype(jnp.float32)
    return jnp.einsum("abt,t->ab", one_hot, weights, precision=HIGHEST)


def short_forces(padded, smooth_taps, deriv_taps):
    smooth_rows = band_matrix(smooth_taps, 48, 16, 0, 0)
    deriv_rows = band_matrix(deriv_taps, 48, 16, 0, 0)
    smooth_x = jnp.einsum("jyz,ji->iyz", padded, smooth_rows, precision=HIGHEST)
    deriv_x = jnp.einsum("jyz,ji->iyz", padded, deriv_rows, precision=HIGHEST)
    smooth_cols = band_matrix(smooth_taps, 80, 48, 0, 0)
    deriv_cols = band_matrix(deriv_taps, 80, 48, 0, 0)
    smooth_depth = band_matrix(smooth_taps, 128, 128, RADIUS, 128)
    deriv_depth = band_matrix(deriv_taps, 128, 128, RADIUS, 128)
    first = jnp.einsum("xjz,ji->xiz", deriv_x, smooth_cols, precision=HIGHEST)
    second = jnp.einsum("xjz,ji->xiz", smooth_x, deriv_cols, precision=HIGHEST)
    third = jnp.einsum("xjz,ji->xiz", smooth_x, smooth_cols, precision=HIGHEST)
    return jnp.stack(
        [
            jnp.einsum("xyj,ji->xyi", first, smooth_depth, precision=HIGHEST),
            jnp.einsum("xyj,ji->xyi", second, smooth_depth, precision=HIGHEST),
            jnp.einsum("xyj,ji->xyi", third, deriv_depth, precision=HIGHEST),
        ]
    )


def per_device(density, momenta, smooth_taps, deriv_taps, kick_step):
    padded, long_range = exchange(density, lax.axis_size("gx"))
    short_range = short_forces(padded, smooth_taps, deriv_taps)
    long_rows = jnp.broadcast_to(long_range[:, :, None], (3, 4, FACTOR, 48, 128)).reshape(3, 16, 48, 128)
    return momenta + kick_step * (short_range + long_rows)


def solution(mesh):
    in_specs = (P("gx", "gy", None), P(None, "gx", "gy", None), P(), P(), P())
    out_specs = P(None, "gx", "gy", None)
    return jax.shard_map(
        per_device, mesh=mesh, in_specs=in_specs, out_specs=out_specs, check_vma=False
    )
```

profile of v0, /device:TPU:1, one launch (start us, length us, event | category | flops | bytes accessed | tf_op | source)
XLA Modules:
  0.0 66.0 jit_solution(7403108865841922747)
XLA Ops:
  0.7 0.0 copy-start.3
  0.7 1.1 %select_reduce_fusion.1 = (f32[48,16]{1,0:T(8,128)S(1)}, f32[48,16]{1,0:T(8,128)S(1)}) fusion(f32[33]{0:T(128)} %param.10, s32[48,16]{1,0:T(8,128)S(1)} %iota_subtract_fusion, f32[33]{0:T(128)} %param.9), kind=kLoop, calls=%fused_computation.26 | loop fusion | flops 125184 | bytes 9480
  1.8 0.1 iota_compare_fusion.1
  2.0 1.0 %fusion.13 = f32[1,80,48]{1,0,2:T(1,128)S(1)} fusion(pred[80,48,33]{0,1,2:T(8,128)(4,1)S(1)} %iota_compare_fusion.1, f32[33]{0:T(128)} %param.10), kind=kOutput, calls=%fused_computation.23 | convolution fusion | flops 1647360 | bytes 142212 | tf_op jit(solution)/shard_map/abt,t->ab/dot_general | solution.py:333
  3.0 1.0 %fusion.14 = f32[1,80,48]{1,0,2:T(1,128)S(1)} fusion(pred[80,48,33]{0,1,2:T(8,128)(4,1)S(1)} %iota_compare_fusion.1, f32[33]{0:T(128)} %param.9), kind=kOutput, calls=%fused_computation.24 | convolution fusion | flops 1647360 | bytes 142212 | tf_op jit(solution)/shard_map/abt,t->ab/dot_general | solution.py:333
  4.0 0.0 copy-start.4
  4.0 0.3 iota_compare_fusion
  4.3 0.0 copy-done.3
  4.3 1.3 %fusion = f32[1,128,128]{2,0,1:T(1,128)S(1)} fusion(pred[128,128,33]{1,0,2:T(32,128)(4,1)S(1)} %iota_compare_fusion, f32[33]{0:T(128)S(1)} %copy-done.3), kind=kOutput, calls=%fused_computation | convolution fusion | flops 6488064 | bytes 606340 | tf_op jit(solution)/shard_map/abt,t->ab/dot_general | solution.py:333
  5.6 1.3 %fusion.2 = f32[1,128,128]{2,0,1:T(1,128)S(1)} fusion(pred[128,128,33]{1,0,2:T(32,128)(4,1)S(1)} %iota_compare_fusion, f32[33]{0:T(128)S(1)} %copy-done.4), kind=kOutput, calls=%fused_computation.2 | convolution fusion | flops 6488064 | bytes 606340 | tf_op jit(solution)/shard_map/abt,t->ab/dot_general | solution.py:333
  7.0 48.7 %shard_map.73 = (f32[48,80,128]{2,1,0:T(8,128)}, f32[3,4,48,128]{3,2,1,0:T(8,128)}) custom-call(f32[16,48,128]{2,1,0:T(8,128)} %density.1, f32[1120,128]{1,0:T(8,128)} %constant.24.clone.cst_hbm, f32[32,184,128]{2,1,0:T(8,128)} %constant.25.clone.tab_hbm), custom_call_target="tpu_custom_call" | custom-call | tf_op jit(solution)/shard_map/pallas_call | solution.py:308
  55.6 3.2 %fusion.4 = f32[16,80,128]{2,0,1:T(8,128)S(1)} fusion(f32[48,80,128]{2,1,0:T(8,128)} %get-tuple-element.7, f32[48,16]{1,0:T(8,128)S(1)} %get-tuple-element.10), kind=kOutput, calls=%fused_computation.5 | convolution fusion | flops 94371840 | bytes 2624512 | tf_op jit(solution)/shard_map/jyz,ji->iyz/dot_general | solution.py:339
  58.9 0.0 copy-done
  58.9 1.6 %fusion.6 = f32[16,80,128]{2,0,1:T(8,128)S(1)} fusion(f32[48,80,128]{2,1,0:T(8,128)S(1)} %copy-done, f32[48,16]{1,0:T(8,128)S(1)} %get-tuple-element.9), kind=kOutput, calls=%fused_computation.7 | convolution fusion | flops 94371840 | bytes 2624512 | tf_op jit(solution)/shard_map/jyz,ji->iyz/dot_general | solution.py:340
  60.4 0.7 %convolution_bitcast_fusion.5 = f32[16,48,128]{2,1,0:T(8,128)S(1)} fusion(f32[80,48,1]{0,1,2:T(8,128)S(1)} %bitcast.64, f32[16,80,128]{2,0,1:T(8,128)S(1)} %fusion.6), kind=kOutput, calls=%fused_computation.14 | convolution fusion | flops 94371840 | bytes 1063936 | tf_op jit(solution)/shard_map/xjz,ji->xiz/dot_general | solution.py:345
  61.1 0.5 convolution_bitcast_fusion.4
  61.6 0.7 %convolution_bitcast_fusion.1 = f32[16,48,128]{2,1,0:T(8,128)S(1)} fusion(f32[80,48,1]{0,1,2:T(8,128)S(1)} %bitcast.65, f32[16,80,128]{2,0,1:T(8,128)S(1)} %fusion.4), kind=kOutput, calls=%fused_computation.10 | convolution fusion | flops 94371840 | bytes 1063936 | tf_op jit(solution)/shard_map/xjz,ji->xiz/dot_general | solution.py:347
  62.3 0.7 %convolution_bitcast_fusion.3 = f32[16,48,128]{2,1,0:T(8,128)S(1)} fusion(f32[80,48,1]{0,1,2:T(8,128)S(1)} %bitcast.67, f32[16,80,128]{2,0,1:T(8,128)S(1)} %fusion.4), kind=kOutput, calls=%fused_computation.12 | convolution fusion | flops 94371840 | bytes 1063936 | tf_op jit(solution)/shard_map/xjz,ji->xiz/dot_general | solution.py:346
  63.0 0.5 convolution_bitcast_fusion.2
  63.5 0.0 copy-start.1
  63.5 0.5 convolution_bitcast_fusion
  64.0 0.1 broadcast_in_dim.2
  64.0 0.7 %copy-done.1 = f32[3,16,48,128]{3,2,1,0:T(8,128)S(1)} copy-done((f32[3,16,48,128]{3,2,1,0:T(8,128)S(1)}, f32[3,16,48,128]{3,2,1,0:T(8,128)}, u32[]{:S(2)}) %copy-start.1) | copy-done | bytes 1179672
  64.7 1.2 %fusion.9 = f32[3,16,48,128]{3,2,1,0:T(8,128)} fusion(f32[3,16,48,128]{3,2,1,0:T(8,128)S(1)} %copy-done.1, f32[3,16,48,128]{3,2,1,0:T(8,128)S(1)} %bitcast.61, f32[1,16,48,128]{3,2,1,0:T(8,128)S(1)} %convolution_bitcast_fusion, f32[1,16,48,128]{3,2,1,0:T(8,128)S(1)} %convolution_bitcast_fusion.2, f32[1,16,48,128]{3,2,1,0:T(8,128)S(1)} %convolution_bitcast_fusion.4, ...), kind=kLoop, calls=%fused_computation.17 | loop fusion | flops 1474560 | bytes 4718596 | tf_op jit(solution)/shard_map/add | solution.py:361
  (7 shorter events, 0.1 us)
Async XLA Ops:
  0.7 3.6 %copy-start.3 = (f32[33]{0:T(128)S(1)}, f32[33]{0:T(128)}, u32[]{:S(2)}) copy-start(f32[33]{0:T(128)} %param.10) | copy-start | bytes 400
  4.0 1.7 %copy-start.4 = (f32[33]{0:T(128)S(1)}, f32[33]{0:T(128)}, u32[]{:S(2)}) copy-start(f32[33]{0:T(128)} %param.9) | copy-start | bytes 400
  55.6 3.3 %copy-start = (f32[48,80,128]{2,1,0:T(8,128)S(1)}, f32[48,80,128]{2,1,0:T(8,128)}, u32[]{:S(2)}) copy-start(f32[48,80,128]{2,1,0:T(8,128)} %get-tuple-element.7) | copy-start | bytes 5898244
  62.3 1.7 %copy-start.2 = (f32[3,4,48,128]{3,2,1,0:T(8,128)S(1)}, f32[3,4,48,128]{3,2,1,0:T(8,128)}, u32[]{:S(2)}) copy-start(f32[3,4,48,128]{3,2,1,0:T(8,128)} %get-tuple-element.8) | copy-start | bytes 884740
  63.5 1.3 %copy-start.1 = (f32[3,16,48,128]{3,2,1,0:T(8,128)S(1)}, f32[3,16,48,128]{3,2,1,0:T(8,128)}, u32[]{:S(2)}) copy-start(f32[3,16,48,128]{3,2,1,0:T(8,128)} %param.8) | copy-start | bytes 3538948
where the time goes:
time: 66.2 us; the launch traced here: 66 us
  Pallas kernels  48.7 us (74%)
  matrix products  12.8 us (19%)
  other arithmetic  2.81 us (4%)
  between operations  0.85 us (1%)
  local copies, waits for them, and re-layouts  0.8 us (1%)
    pallas_call x1, Pallas kernels, exchange(): pl.pallas_call(functools.partial(kernel, gx_count), out_shape=(jax.ShapeD...  48.7 us
    dot_general x4, matrix products, band_matrix(): return jnp.einsum('abt,t->ab', one_hot, weights, precision=HIGHEST)  4.63 us
    dot_general x1, matrix products, short_forces(): smooth_x = jnp.einsum('jyz,ji->iyz', padded, smooth_rows, precision=HIGHEST)  3.24 us
    dot_general x1, matrix products, short_forces(): deriv_x = jnp.einsum('jyz,ji->iyz', padded, deriv_rows, precision=HIGHEST)  1.56 us

commit v1 on v0

v1 whole, which is shorter than its diff:
```python
import functools
import math

import jax
import jax.numpy as jnp
import numpy as np
from jax import lax
from jax.experimental import pallas as pl
from jax.experimental.pallas import tpu as pltpu
from jax.sharding import PartitionSpec as P

FACTOR = 4
RADIUS = 16
LONG_COUPLING = 16.0
HIGHEST = lax.Precision.HIGHEST
MESH = pl.DeviceIdType.MESH
F32 = jnp.float32

T_P, T_Q, T_A, T_B, T_G, T_W, T_ROWS = 0, 8, 16, 32, 48, 72, 80
C_ZF, C_ZI, C_ZD, C_YF, C_YI, C_ROWS = 0, 32, 64, 96, 608, 1120


def z_basis():
    n = np.arange(32)
    basis = np.zeros((2, 16, 32))
    norm = np.full((2, 16), 2.0 / 32)
    for g in range(16):
        basis[0, g] = np.cos(2 * np.pi * g * n / 32)
        basis[1, g] = np.sin(2 * np.pi * g * n / 32)
    basis[1, 0] = np.cos(np.pi * n)
    norm[:, 0] = 1.0 / 32
    return basis.reshape(32, 32), norm.reshape(32)


def y_basis(count):
    half = count // 2
    wave = np.array([m if m <= half else m - half for m in range(count)])
    y = np.arange(count)
    angle = 2 * np.pi / count * (wave[:, None] * y[None, :] % count)
    is_cos = (np.arange(count) <= half)[:, None]
    basis = np.where(is_cos, np.cos(angle), np.sin(angle))
    norm = np.where((wave == 0) | (wave == half), 1.0, 2.0) / count
    return basis, norm, wave


def shared_constants():
    out = np.zeros((C_ROWS, 128))
    zb, zn = z_basis()
    out[C_ZF : C_ZF + 32] = np.repeat(zb, 4, axis=1) / 64.0
    zi = zb * zn[:, None] * LONG_COUPLING
    out[C_ZI : C_ZI + 32] = np.repeat(zi, 4, axis=1)
    zd = 0.5 * (np.roll(zi, -1, axis=1) - np.roll(zi, 1, axis=1))
    out[C_ZD : C_ZD + 32] = np.repeat(zd, 4, axis=1)
    yb, yn, _ = y_basis(192)
    for tile in range(2):
        for half in range(2):
            fwd = np.zeros((128, 128))
            inv = np.zeros((128, 128))
            fwd[:96, :96] = yb[96 * half : 96 * half + 96, 96 * tile : 96 * tile + 96].T
            for jj in range(8):
                for p in range(14):
                    y = (12 * (8 * tile + jj) - 1 + p) % 192
                    cols = slice(96 * half, 96 * half + 96)
                    inv[:96, 16 * jj + p] = yb[cols, y] * yn[cols]
            row = C_YF + (2 * tile + half) * 128
            out[row : row + 128] = fwd
            row = C_YI + (2 * half + tile) * 128
            out[row : row + 128] = inv
    return out.astype(np.float32)


def solve_tables(chips):
    n = 8 * chips
    out = np.zeros((17, 2, T_ROWS, 128))
    _, _, wave = y_basis(192)
    for kz in range(17):
        for half in range(2):
            t = out[kz, half]
            ky = wave[96 * half : 96 * half + 96]
            a = np.ones(128)
            a[:96] = (2 - 2 * np.cos(2 * np.pi * ky / 192)) + (2 - 2 * np.cos(2 * np.pi * kz / 32))
            zero = np.zeros(128, bool)
            zero[:96] = (ky == 0) & (kz == 0)
            a[zero] = 1.0
            r = 1 + a / 2 - np.sqrt(a + a * a / 4)
            den = (1 / r - r) * (1 - r**n)
            pick = lambda general, special: np.where(zero, special, general)
            for x8 in range(8):
                t[T_P + x8] = pick(r ** float(-x8), 1.0)
                t[T_Q + x8] = pick(r**x8, float(x8))
            for o in range(10):
                x8 = o - 1
                t[T_A + o] = pick(r ** float(x8) / den, -x8 / 2 + x8 * x8 / (2 * n))
                t[T_B + o] = pick(r ** float(-x8) / den, -x8 / n)
            for o in range(17):
                d = abs(o - 8)
                t[T_G + o] = pick((r**d + r ** (n - d)) / den, -d * (n - d) / (2 * n))
            t[T_W] = pick(r**8, 1.0)
    return out.astype(np.float32)


def dot(a, b):
    return lax.dot_general(a, b, (((1,), (0,)), ((), ())), precision=HIGHEST, preferred_element_type=F32)


def dot_nt(a, b):
    return lax.dot_general(a, b, (((1,), (1,)), ((), ())), precision=HIGHEST, preferred_element_type=F32)


def wrap(value, count):
    return lax.rem(value + count, count)


def send_order(chips):
    ring = min(16, chips)
    def hops(step):
        along = step % ring
        return min(along, ring - along) + (2 if step >= ring else 0)
    return sorted(range(1, chips), key=lambda step: (-hops(step), step))


def band_rows(taps, rows, shift):
    lane = lax.broadcasted_iota(jnp.int32, (1, 128), 1)
    row = jnp.zeros((1, 128), F32)
    for tap in range(2 * RADIUS + 1):
        row = jnp.where(lane == tap, taps[tap], row)
    return pltpu.roll(jnp.broadcast_to(row, (rows, 128)), shift % 128, 1, stride=1, stride_axis=0)


def convolve_rows(padded, mid, smooth, deriv, first):
    for group in range(0, 16, 8):
        sums = [[None] * 8, [None] * 8]
        for tap in range(2 * RADIUS + 1):
            weights = (smooth[tap], deriv[tap])
            for i in range(8):
                cells = padded[group + i + tap, pl.ds(first, 8), :]
                for f in range(2):
                    term = cells * weights[f]
                    sums[f][i] = term if tap == 0 else sums[f][i] + term
        for f in range(2):
            for i in range(8):
                mid[f, group + i, pl.ds(first, 8), :] = sums[f][i]


NEAR_LAST = (8, 7, 9, 6, 10, 5, 11, 4, 12, 3, 13, 2, 14, 1, 15)


def kernel(
    gx_count, smooth, deriv, kick, density, momenta, cst_hbm, tab_hbm, out,
    padded, mid, bands, cst, tab, m1, r1, fs, pair, mom, r2, os_, pair2, ps, r3,
    load_sem, strip_send, strip_recv, tile_send, tile_recv, corner_send, corner_recv,
    m_send, m_recv, p_send, p_recv,
):
    gx = lax.axis_index("gx")
    gy = lax.axis_index("gy")
    chips = gx_count // 2
    core = lax.rem(gx, 2)
    chip = gx // 2
    partner = gx + 1 - 2 * core
    outer = wrap(gx + 2 * core - 1, gx_count)

    barrier = pltpu.get_barrier_semaphore()

    def greet(device):
        pl.semaphore_signal(barrier, inc=1, device_id=device, device_id_type=MESH)

    for step in send_order(chips):
        greet({"gx": 2 * lax.rem(chip + step, chips) + core})
    for step in NEAR_LAST:
        greet({"gy": lax.rem(gy + step, 16)})
    greet({"gx": outer})
    greet({"gx": partner})

    is_zero = (gy == 0).astype(jnp.int32)
    loads = [
        pltpu.make_async_copy(density, padded.at[16:32, 16:64], load_sem.at[0]),
        pltpu.make_async_copy(cst_hbm, cst, load_sem.at[1]),
        pltpu.make_async_copy(tab_hbm.at[gy, core], tab.at[0], load_sem.at[2]),
        pltpu.make_async_copy(tab_hbm.at[gy + 16 * is_zero, core], tab.at[1], load_sem.at[3]),
    ]
    for load in loads:
        load.start()
    load_momenta = pltpu.make_async_copy(momenta, out, load_sem.at[4])
    load_momenta.start()
    bands[0:48] = band_rows(smooth, 48, 0)
    bands[48:96] = band_rows(deriv, 48, 0)
    bands[96:224] = band_rows(smooth, 128, -RADIUS)
    bands[224:352] = band_rows(deriv, 128, -RADIUS)
    for load in loads:
        load.wait()

    lane = lax.broadcasted_iota(jnp.int32, (48, 128), 1)
    block = lax.broadcasted_iota(jnp.int32, (48, 128), 0) // 4
    placed = (lane == block + 12 * lax.rem(gy, 8)).astype(F32)
    zf = cst[C_ZF : C_ZF + 32]
    for xl in range(4):
        rows = padded[16 + 4 * xl, 16:64]
        for fine in range(1, 4):
            rows = rows + padded[16 + 4 * xl + fine, 16:64]
        spread = dot(dot_nt(zf, rows), placed)
        for c in range(2):
            m1[:, c * 4 + xl, :] = spread[16 * c : 16 * c + 16]

    pl.semaphore_wait(barrier, (chips - 1) + 15 + 2)

    def remote(src, dst, send_sem, recv_sem, device):
        return pltpu.make_async_remote_copy(
            src_ref=src, dst_ref=dst, send_sem=send_sem, recv_sem=recv_sem,
            device_id=device, device_id_type=MESH,
        )

    for step in NEAR_LAST:
        target = lax.rem(gy + step, 16)
        remote(m1.at[target], r1.at[gy], m_send.at[0], m_recv.at[0], {"gy": target}).start()
    below, above = wrap(gy - 1, 16), lax.rem(gy + 1, 16)
    strips = [
        remote(padded.at[16:32, 16:32], padded.at[16:32, 64:80], strip_send.at[0], strip_recv.at[0], {"gy": below}),
        remote(padded.at[16:32, 48:64], padded.at[16:32, 0:16], strip_send.at[1], strip_recv.at[1], {"gy": above}),
    ]
    back, ahead = wrap(gx - 1, gx_count), lax.rem(gx + 1, gx_count)
    tiles = [
        remote(padded.at[16:32, 16:64], padded.at[32:48, 16:64], tile_send.at[0], tile_recv.at[0], {"gx": back}),
        remote(padded.at[16:32, 16:64], padded.at[0:16, 16:64], tile_send.at[1], tile_recv.at[1], {"gx": ahead}),
    ]
    for copy in strips + tiles:
        copy.start()

    r1[gy] = m1[gy]
    pltpu.make_async_copy(r1.at[0:15], r1.at[0:15], m_recv.at[0]).wait()
    low = r1[0]
    high = r1[8]
    for j in range(1, 8):
        low = low + r1[j]
        high = high + r1[8 + j]
    for half in range(2):
        first = C_YF + half * 128
        second = C_YF + (2 + half) * 128
        fs[half] = dot(low, cst[first : first + 128]) + dot(high, cst[second : second + 128])
    swap = remote(fs.at[1 - core], pair.at[core], p_send.at[0], p_recv.at[0], {"gx": partner})
    swap.start()
    pair[core] = fs[core]
    swap.wait_recv()

    e0 = pair[0]
    e1 = pair[1]
    for pq, table in ((0, T_P), (1, T_Q)):
        for c in range(2):
            rows = slice(4 * c, 4 * c + 4)
            terms = e0[rows] * tab[c, table : table + 4] + e1[rows] * tab[c, table + 4 : table + 8]
            mom[2 * pq + c : 2 * pq + c + 1, :] = jnp.sum(terms, axis=0, keepdims=True)
    for step in send_order(chips):
        target = 2 * lax.rem(chip + step, chips) + core
        remote(mom, r2.at[step], m_send.at[1], m_recv.at[1], {"gx": target}).start()

    for copy in strips:
        copy.wait_recv()
    corners = []
    for side, cols in enumerate((slice(0, 16), slice(64, 80))):
        corners.append(remote(padded.at[16:32, cols], padded.at[32:48, cols], corner_send.at[2 * side], corner_recv.at[2 * side], {"gx": back}))
        corners.append(remote(padded.at[16:32, cols], padded.at[0:16, cols], corner_send.at[2 * side + 1], corner_recv.at[2 * side + 1], {"gx": ahead}))
    for copy in corners:
        copy.start()
    for copy in tiles:
        copy.wait_recv()

    @pl.loop(2, 8)
    def _(k):
        convolve_rows(padded, mid, smooth, deriv, pl.multiple_of(8 * k, 8))

    pltpu.make_async_copy(r2.at[1:chips], r2.at[1:chips], m_recv.at[1]).wait()
    ratio = jnp.concatenate([tab[c, T_W : T_W + 1] for c in (0, 1, 0, 1)], axis=0)
    is_first = lax.broadcasted_iota(jnp.int32, (4, 128), 0) < 2
    total = jnp.zeros((4, 128), F32)
    ramp = jnp.zeros((4, 128), F32)
    for step in range(chips - 1, 0, -1):
        total = (total + jnp.where(is_first, r2[step], r2[chips - step])) * ratio
        ramp = ramp + total
    is_mean = (gy == 0) & (core == 0)
    row8 = lax.broadcasted_iota(jnp.int32, (8, 128), 0)
    lane8 = lax.broadcasted_iota(jnp.int32, (8, 128), 1)
    for ct in range(2):
        for c in range(2):
            o = 4 * ct
            phi = (
                tab[c, T_A + o : T_A + o + 8] * total[c : c + 1]
                + tab[c, T_B + o : T_B + o + 8] * total[2 + c : 3 + c]
            )
            if c == 0:
                weight = jnp.where((lane8 == 0) & is_mean, (row8 + (o - 1)).astype(F32) * (1.0 / chips), 0.0)
                phi = phi + weight * ramp[0:1]
            for x8 in range(8):
                source = (e0 if x8 < 4 else e1)[c * 4 + x8 % 4 : c * 4 + x8 % 4 + 1]
                start = T_G + 7 + o - x8
                phi = phi + tab[c, start : start + 8] * source
            os_[ct, c * 8 : c * 8 + 8, :] = phi
    swap2 = remote(os_.at[1 - core], pair2.at[core], p_send.at[1], p_recv.at[1], {"gx": partner})
    swap2.start()
    pair2[core] = os_[core]
    swap2.wait_recv()

    h0 = pair2[0]
    h1 = pair2[1]
    for tile in range(2):
        first = C_YI + tile * 128
        second = C_YI + (2 + tile) * 128
        phi = dot(h0, cst[first : first + 128]) + dot(h1, cst[second : second + 128])
        for odd in range(2):
            parts = [phi[0:8], phi[8:16]]
            parts[1 - odd] = pltpu.roll(parts[1 - odd], 64, 1)
            ps[2 * tile + odd] = jnp.where(lane8 < 64, parts[0], parts[1])
    for step in NEAR_LAST:
        target = lax.rem(gy + step, 16)
        remote(ps.at[target // 4], r3.at[gy], m_send.at[2], m_recv.at[2], {"gy": target}).start()
    r3[gy] = ps[gy // 4]

    for copy in corners:
        copy.wait_recv()

    @pl.loop(0, 4)
    def _(k):
        convolve_rows(padded, mid, smooth, deriv, pl.multiple_of(8 * (k + 6 * (k // 2)), 8))

    load_momenta.wait()
    time_step = kick[0]

    @pl.loop(0, 4)
    def _(k):
        cols = bands[0:96, 0:80]
        firsts, seconds, thirds = [], [], []
        for u in range(4):
            x = 4 * k + u
            firsts.append(dot(cols[0:48], mid[1, x]))
            both = dot(cols, mid[0, x])
            thirds.append(both[0:48])
            seconds.append(both[48:96])
        smoothed = dot_nt(jnp.concatenate(firsts + seconds, axis=0), bands[96:224])
        derived = dot_nt(jnp.concatenate(thirds, axis=0), bands[224:352])
        for u in range(4):
            x = 4 * k + u
            out[0, x] = out[0, x] + time_step * smoothed[48 * u : 48 * u + 48]
            out[1, x] = out[1, x] + time_step * smoothed[48 * (4 + u) : 48 * (4 + u) + 48]
            out[2, x] = out[2, x] + time_step * derived[48 * u : 48 * u + 48]

    here = block + 16 * lax.rem(gy, 4) + 1
    at_cell = (lane == here).astype(F32)
    slope = 0.5 * (lane == here + 1).astype(F32) - 0.5 * (lane == here - 1).astype(F32)
    zi = cst[C_ZI : C_ZI + 32] * time_step
    zd = cst[C_ZD : C_ZD + 32] * time_step
    pltpu.make_async_copy(r3.at[0:15], r3.at[0:15], m_recv.at[2]).wait()
    along = []
    across = []
    for i in range(6):
        tile = r3[:, i, :]
        coeffs = jnp.concatenate([tile, pltpu.roll(tile, 64, 1)], axis=0)
        along.append(dot_nt(at_cell, coeffs))
        if 1 <= i <= 4:
            across.append(dot_nt(slope, coeffs))
    for xl in range(4):
        for d, force in enumerate((
            dot(0.5 * (along[xl + 2] - along[xl]), zi),
            dot(across[xl], zi),
            dot(along[xl + 1], zd),
        )):
            for fine in range(4):
                out[d, 4 * xl + fine] = out[d, 4 * xl + fine] + force

    for copy in strips + tiles + corners + [swap, swap2]:
        copy.wait_send()
    pltpu.make_async_copy(m1.at[0:15], m1.at[0:15], m_send.at[0]).wait()
    pltpu.make_async_copy(r2.at[1:chips], r2.at[1:chips], m_send.at[1]).wait()
    pltpu.make_async_copy(r3.at[0:15], r3.at[0:15], m_send.at[2]).wait()


def per_device(density, momenta, smooth_taps, deriv_taps, kick_step):
    gx_count = lax.axis_size("gx")
    chips = gx_count // 2
    any_spec = pl.BlockSpec(memory_space=pl.ANY)
    vmem_spec = pl.BlockSpec(memory_space=pltpu.VMEM)
    smem_spec = pl.BlockSpec(memory_space=pltpu.SMEM)
    vm = lambda *shape: pltpu.VMEM(shape, F32)
    dma = lambda n: pltpu.SemaphoreType.DMA((n,))
    return pl.pallas_call(
        functools.partial(kernel, gx_count),
        out_shape=pltpu.VMEM((3, 16, 48, 128), F32),
        in_specs=[smem_spec] * 3 + [any_spec] * 4,
        out_specs=vmem_spec,
        scratch_shapes=[
            vm(48, 80, 128), vm(2, 16, 80, 128), vm(352, 128),
            vm(C_ROWS, 128), vm(2, T_ROWS, 128), vm(16, 8, 128), vm(16, 8, 128), vm(2, 8, 128), vm(2, 8, 128),
            vm(4, 128), vm(chips, 4, 128), vm(2, 16, 128), vm(2, 16, 128), vm(4, 8, 128), vm(16, 8, 128),
            dma(5), dma(2), dma(2), dma(2), dma(2), dma(4), dma(4), dma(3), dma(3), dma(2), dma(2),
        ],
        compiler_params=pltpu.CompilerParams(collective_id=0, has_side_effects=True),
    )(
        smooth_taps, deriv_taps, kick_step.reshape(1), density, momenta,
        jnp.asarray(shared_constants()), jnp.asarray(solve_tables(chips)),
    )


def solution(mesh):
    in_specs = (P("gx", "gy", None), P(None, "gx", "gy", None), P(), P(), P())
    out_specs = P(None, "gx", "gy", None)
    return jax.shard_map(
        per_device, mesh=mesh, in_specs=in_specs, out_specs=out_specs, check_vma=False
    )
```

time: 66.2 us -> 50.1 us (0.76)
  matrix products: 12.8 us -> 0 us
  other arithmetic: 2.81 us -> 0 us
    dot_general x12 -> x0, matrix products: 12.8 us -> none  [the longest x4 4.63 us: band_matrix(): return jnp.einsum('abt,t->ab', one_hot, weights, precision=HIGHEST)]
    add x1 -> x0, other arithmetic: 1.23 us -> none  [per_device(): return momenta + kick_step * (short_range + long_rows)]
    unnamed x1 -> x0, other arithmetic: 1.11 us -> none
where the time goes in v1:
time: 50.1 us; the launch traced here: 49.9 us
  Pallas kernels  48.2 us (96%)
  local copies, waits for them, and re-layouts  1.02 us (2%)
  between operations  0.66 us (1%)
    pallas_call x1, Pallas kernels, per_device(): pl.pallas_call(functools.partial(kernel, gx_count), out_shape=pltpu.VMEM(...  48.2 us
    unnamed x1, local copies, waits for them, and re-layouts  1.02 us

profile of v1, /device:TPU:1, one launch (start us, length us, event | category | flops | bytes accessed | tf_op | source)
XLA Modules:
  0.0 49.9 jit_solution(10419765970801371451)
XLA Ops:
  0.7 48.2 %shard_map.73 = f32[3,16,48,128]{3,2,1,0:T(8,128)S(1)} custom-call(f32[33]{0:T(128)} %smooth.1, f32[33]{0:T(128)} %deriv.1, f32[1]{0:T(128)} %bitcast.1.kick, f32[16,48,128]{2,1,0:T(8,128)} %density.1, f32[3,16,48,128]{3,2,1,0:T(8,128)} %momenta.1, f32[1120,128]{1,0:T(8,128)} %constant.4.clone.cst_hbm, f32[17,2,80,128]{3,2,1,0:T(8,128)} %constant.5.clone.tab_hbm), custom_call_target="tpu_custom_call" | custom-call | tf_op jit(solution)/shard_map/pallas_call | solution.py:382
  48.9 1.0 %copy.9 = f32[3,16,48,128]{3,2,1,0:T(8,128)} copy(f32[3,16,48,128]{3,2,1,0:T(8,128)S(1)} %shard_map.73) | data formatting | bytes 2359296

commit v2 on v1

--- a/solution.py
+++ b/solution.py
@@ -270,12 +270,16 @@
     pltpu.make_async_copy(r2.at[1:chips], r2.at[1:chips], m_recv.at[1]).wait()
     ratio = jnp.concatenate([tab[c, T_W : T_W + 1] for c in (0, 1, 0, 1)], axis=0)
     is_first = lax.broadcasted_iota(jnp.int32, (4, 128), 0) < 2
+    is_mean = (gy == 0) & (core == 0)
+    lane1 = lax.broadcasted_iota(jnp.int32, (1, 128), 1)
+    level = jnp.where((lane1 == 0) & is_mean, mom[0:1, :] * 0.125, 0.0)
+    none = jnp.zeros((1, 128), F32)
+    uniform = jnp.concatenate([8.0 * level, none, 28.0 * level, none], axis=0)
     total = jnp.zeros((4, 128), F32)
     ramp = jnp.zeros((4, 128), F32)
     for step in range(chips - 1, 0, -1):
-        total = (total + jnp.where(is_first, r2[step], r2[chips - step])) * ratio
+        total = (total + (jnp.where(is_first, r2[step], r2[chips - step]) - uniform)) * ratio
         ramp = ramp + total
-    is_mean = (gy == 0) & (core == 0)
     row8 = lax.broadcasted_iota(jnp.int32, (8, 128), 0)
     lane8 = lax.broadcasted_iota(jnp.int32, (8, 128), 1)
     for ct in range(2):
@@ -290,6 +294,8 @@
                 phi = phi + weight * ramp[0:1]
             for x8 in range(8):
                 source = (e0 if x8 < 4 else e1)[c * 4 + x8 % 4 : c * 4 + x8 % 4 + 1]
+                if c == 0:
+                    source = source - level
                 start = T_G + 7 + o - x8
                 phi = phi + tab[c, start : start + 8] * source
             os_[ct, c * 8 : c * 8 + 8, :] = phi

time: 50.1 us -> 50.1 us (level)
  no operation moved by 1% of the time
where the time goes in v2:
time: 50.1 us; the launch traced here: 49.9 us
  Pallas kernels  48.2 us (96%)
  local copies, waits for them, and re-layouts  1.02 us (2%)
  between operations  0.66 us (1%)
    pallas_call x1, Pallas kernels, per_device(): pl.pallas_call(functools.partial(kernel, gx_count), out_shape=pltpu.VMEM(...  48.2 us
    unnamed x1, local copies, waits for them, and re-layouts  1.02 us

profile of v2, /device:TPU:1, one launch (start us, length us, event | category | flops | bytes accessed | tf_op | source)
XLA Modules:
  0.0 49.9 jit_solution(7016597950465573488)
XLA Ops:
  0.7 48.2 %shard_map.73 = f32[3,16,48,128]{3,2,1,0:T(8,128)S(1)} custom-call(f32[33]{0:T(128)} %smooth.1, f32[33]{0:T(128)} %deriv.1, f32[1]{0:T(128)} %bitcast.1.kick, f32[16,48,128]{2,1,0:T(8,128)} %density.1, f32[3,16,48,128]{3,2,1,0:T(8,128)} %momenta.1, f32[1120,128]{1,0:T(8,128)} %constant.4.clone.cst_hbm, f32[17,2,80,128]{3,2,1,0:T(8,128)} %constant.5.clone.tab_hbm), custom_call_target="tpu_custom_call" | custom-call | tf_op jit(solution)/shard_map/pallas_call | solution.py:388
  48.9 1.0 %copy.9 = f32[3,16,48,128]{3,2,1,0:T(8,128)} copy(f32[3,16,48,128]{3,2,1,0:T(8,128)S(1)} %shard_map.73) | data formatting | bytes 2359296
